TPU v7x, 16 devices: a 4x2x1 block of a 4x4x8 slice. The times are simulated.
16 devices in a mesh: dp: 2 (over y, z), ep: 8 (over x, core).
Axes of the slice: x: 4, y: 2, z: 1, core: 2. Of those that a mesh axis runs over, the one named last changes fastest.
The devices are a block of a 4x4x8 slice.
Arguments:
- x: bfloat16 [2, 8, 256, 4096], P('dp', 'ep'), parts along dimension 0
- expert: int32 [2, 8, 256, 8], P('dp', 'ep'), parts along dimension 0
- slot: int32 [2, 8, 256, 8], P('dp', 'ep'), parts along dimension 0
- gate: float32 [2, 8, 256, 8], P('dp', 'ep'), parts along dimension 0
- w_gate: bfloat16 [64, 4096, 1536], P('ep')
- w_up: bfloat16 [64, 4096, 1536], P('ep')
- w_down: bfloat16 [64, 1536, 4096], P('ep')
Outputs:
- y: bfloat16 [2, 8, 256, 4096], P('dp', 'ep'), parts along dimension 0
There are 2 independent parts. A program takes and returns all parts, laid end to end along the dimension named above; an argument that names none is the same for every part.
All inputs are finite; a program needn't handle non-finite values.
Results may differ from a plain program's by a relative error of at most 0.009.
Values are sent between devices in bfloat16 or wider.
A program may use at most 768 MiB of HBM per device.

v0:
```python
import jax
import jax.numpy as jnp
from jax import lax
from jax.sharding import NamedSharding, PartitionSpec as P


def einsum(form, a, b):
    return jnp.einsum(form, a.astype(jnp.float32), b.astype(jnp.float32))


def solution(mesh):
    def placed(v, *spec):
        return lax.with_sharding_constraint(v, NamedSharding(mesh, P(*spec)))

    def step(x, expert, slot, gate, w_gate, w_up, w_down):
        experts, (tokens, top) = w_gate.shape[0], expert.shape[2:]
        slots = 5 * tokens * top // (4 * experts)
        to_expert = jax.nn.one_hot(expert, experts, dtype=jnp.bfloat16)
        to_slot = jax.nn.one_hot(slot, slots, dtype=jnp.bfloat16)
        weighted = to_expert * gate[..., None].astype(jnp.bfloat16)
        dispatch = einsum("abtke,abtkc->abtec", to_expert, to_slot).astype(jnp.bfloat16)
        combine = einsum("abtke,abtkc->abtec", weighted, to_slot).astype(jnp.bfloat16)
        z = einsum("abtec,abtd->aebcd", dispatch, x).astype(jnp.bfloat16)
        z = placed(z, "dp", None, "ep", None, None)
        z = placed(z, "dp", "ep", None, None, None)
        h = jax.nn.silu(einsum("aebcd,edf->aebcf", z, w_gate))
        h = (h * einsum("aebcd,edf->aebcf", z, w_up)).astype(jnp.bfloat16)
        out = einsum("aebcf,efd->aebcd", h, w_down).astype(jnp.bfloat16)
        out = placed(out, "dp", "ep", None, None, None)
        out = placed(out, "dp", None, "ep", None, None)
        y = einsum("abtec,aebcd->abtd", combine, out)
        return y.astype(jnp.bfloat16)

    return step
```

profile of v0, /device:TPU:112, one launch (start us, length us, event | category | flops | bytes accessed | tf_op | source)
XLA Modules:
  0.0 680.3 jit_solution(1962858264284220713)
XLA Ops:
  0.0 0.0 copy-start
  0.0 1.0 copy.10
  1.0 0.0 copy-start.2
  1.0 0.8 copy.12
  1.8 0.0 copy-done.2
  1.8 0.0 copy-start.4
  1.9 0.6 copy-done.4
  2.5 3.6 convolution_convert_fusion.1
  6.1 5.6 copy.13
  11.7 0.0 copy-done
  11.8 10.2 %convolution_convert_fusion = bf16[64,40,4096]{2,1,0:T(8,128)(2,1)} fusion(bf16[256,64,40]{0,2,1:T(8,128)(2,1)S(1)} %copy.13, bf16[1,1,256,4096]{3,2,1,0:T(8,128)(2,1)S(1)} %copy-done), kind=kOutput, calls=%fused_computation.18 | convolution fusion | flops 5379194880 | bytes 24379392 | tf_op jit(solution)/abtec,abtd->aebcd/dot_general | solution.py:8
  21.9 238.1 %all-to-all.4 = bf16[1,8,8,1,40,4096]{5,4,2,3,0,1:T(8,128)(2,1)} all-to-all(bf16[1,8,8,1,40,4096]{5,4,2,3,0,1:T(8,128)(2,1)} %bitcast.98), channel_id=1, replica_groups=mesh['dp'=2,'ep'=8] {'ep'}, dimensions={1} | all-to-all | bytes 41943040 | tf_op jit(solution)/sharding_constraint;jit(solution)/sharding_constraint | solution.py:13
  260.0 49.2 %fusion.2 = f32[8,8,40,1536]{3,2,1,0:T(8,128)} fusion(bf16[8,4096,1536]{2,1,0:T(8,128)(2,1)} %param.5, bf16[1,8,8,1,40,4096]{5,4,2,3,0,1:T(8,128)(2,1)} %all-to-all.4), kind=kOutput, calls=%fused_computation.2 | convolution fusion | flops 32212254720 | bytes 137363456 | tf_op jit(solution)/aebcd,edf->aebcf/dot_general | solution.py:8
  309.3 49.3 %fusion.4 = f32[8,8,40,1536]{3,2,1,0:T(8,128)} fusion(bf16[8,4096,1536]{2,1,0:T(8,128)(2,1)} %param.4, bf16[1,8,8,1,40,4096]{5,4,2,3,0,1:T(8,128)(2,1)} %all-to-all.4), kind=kOutput, calls=%fused_computation.4 | convolution fusion | flops 32212254720 | bytes 137363456 | tf_op jit(solution)/aebcd,edf->aebcf/dot_general | solution.py:8
  358.5 57.1 %convert_bitcast_fusion = bf16[1,8,8,1,40,4096]{5,4,2,1,3,0:T(8,128)(2,1)} fusion(bf16[8,1536,4096]{2,1,0:T(8,128)(2,1)} %param.6, f32[8,8,40,1536]{3,2,1,0:T(8,128)} %fusion.2, f32[8,8,40,1536]{3,2,1,0:T(8,128)} %fusion.4), kind=kOutput, calls=%fused_computation.8 | convolution fusion | flops 32246333440 | bytes 153092096 | tf_op jit(solution)/aebcf,efd->aebcd/dot_general | solution.py:8
  415.7 17.5 %copy.16 = bf16[1,8,8,1,40,4096]{5,4,1,3,0,2:T(8,128)(2,1)} copy(bf16[1,8,8,1,40,4096]{5,4,2,1,3,0:T(8,128)(2,1)} %convert_bitcast_fusion) | data formatting | bytes 41943040 | tf_op jit(solution)/sharding_constraint;jit(solution)/sharding_constraint | solution.py:13
  433.2 0.0 copy-start.6
  433.2 0.0 copy-start.3
  433.2 0.0 copy-start.5
  433.2 6.7 all-to-all-start.1
  439.8 0.0 copy-done.6
  439.9 0.1 copy.11
  440.0 0.0 copy-done.3
  440.0 0.0 copy-done.5
  440.0 0.0 copy-start.1
  440.0 4.3 convolution_convert_fusion.2
  444.3 5.6 copy.23
  449.9 218.9 %all-to-all-done.1 = bf16[1,8,8,1,40,4096]{5,4,1,3,0,2:T(8,128)(2,1)} async-done(((bf16[1,8,8,1,40,4096]{5,4,1,3,0,2:T(8,128)(2,1)}), bf16[1,8,8,1,40,4096]{5,4,1,3,0,2:T(8,128)(2,1)}, u32[]{:S(2)}, u32[]{:S(2)}) %all-to-all-start.1) | async-done | bytes 20971552 | tf_op jit(solution)/sharding_constraint;jit(solution)/sharding_constraint | solution.py:13
  668.8 11.5 %fusion.19 = bf16[1,1,256,4096]{3,2,1,0:T(8,128)(2,1)} fusion(bf16[256,64,40]{0,2,1:T(8,128)(2,1)S(1)} %copy.23, bf16[64,40,4096]{2,1,0:T(8,128)(2,1)} %bitcast.25), kind=kOutput, calls=%fused_computation.22 | convolution fusion | flops 5369757696 | bytes 24379392 | tf_op jit(solution)/abtec,aebcd->abtd/dot_general | solution.py:8
  680.3 0.0 copy-done.1
  (1 shorter events, 0.0 us)
Async XLA Ops:
  0.0 11.7 %copy-start = (bf16[1,1,256,4096]{3,2,1,0:T(8,128)(2,1)S(1)}, bf16[1,1,256,4096]{3,2,1,0:T(8,128)(2,1)}, u32[]{:S(2)}) copy-start(bf16[1,1,256,4096]{3,2,1,0:T(8,128)(2,1)} %param.3) | copy-start | bytes 6291460
  1.0 0.9 copy-start.2
  1.8 0.7 copy-start.4
  433.2 6.7 copy-start.6
  433.2 6.8 %copy-start.3 = (s32[256,8]{1,0:T(8,128)S(1)}, s32[256,8]{1,0:T(8,128)}, u32[]{:S(2)}) copy-start(s32[256,8]{1,0:T(8,128)} %copy-done.2) | copy-start | bytes 24580
  433.2 6.8 %copy-start.5 = (s32[256,8]{1,0:T(8,128)S(1)}, s32[256,8]{1,0:T(8,128)}, u32[]{:S(2)}) copy-start(s32[256,8]{1,0:T(8,128)} %copy-done.4) | copy-start | bytes 24580
  433.2 235.7 %all-to-all-start.1 = ((bf16[1,8,8,1,40,4096]{5,4,1,3,0,2:T(8,128)(2,1)}), bf16[1,8,8,1,40,4096]{5,4,1,3,0,2:T(8,128)(2,1)}, u32[]{:S(2)}, u32[]{:S(2)}) async-start(bf16[1,8,8,1,40,4096]{5,4,1,3,0,2:T(8,128)(2,1)} %copy.16), calls=%async_computation.1 | async-start | bytes 41943040 | tf_op jit(solution)/sharding_constraint;jit(solution)/sharding_constraint | solution.py:13
  440.0 240.3 %copy-start.1 = (bf16[1,1,256,4096]{3,2,1,0:T(8,128)(2,1)S(1)}, bf16[1,1,256,4096]{3,2,1,0:T(8,128)(2,1)}, u32[]{:S(2)}) copy-start(bf16[1,1,256,4096]{3,2,1,0:T(8,128)(2,1)} %param.3) | copy-start | bytes 6291460
where the time goes:
time: 681 us; the launch traced here: 680 us
  blocking collectives  238 us (35%)
  waiting for transfers between devices  219 us (32%)
  matrix products  185 us (27%)
  local copies, waits for them, and re-layouts  31.3 us (5%)
    another operation x1, blocking collectives, placed(): return lax.with_sharding_constraint(v, NamedSharding(mesh, P(*spec)))  238 us
    another operation x1, waiting for transfers between devices, placed(): return lax.with_sharding_constraint(v, NamedSharding(mesh, P(*spec)))  219 us
    dot_general x7, matrix products, einsum(): return jnp.einsum(form, a.astype(jnp.float32), b.astype(jnp.float32))  185 us
    another operation x1, local copies, waits for them, and re-layouts, placed(): return lax.with_sharding_constraint(v, NamedSharding(mesh, P(*spec)))  17.5 us
  transfers between devices with their start and end apart: 1, of which 1 were waited for; matrix products, arithmetic and copies ran while one was open for 1% of the time, Pallas kernels for 0%

commit v1 on v0

v1 whole, which is shorter than its diff:
```python
import functools

import jax
import jax.numpy as jnp
from jax import lax
from jax.experimental import pallas as pl
from jax.experimental.pallas import tpu as pltpu
from jax.sharding import PartitionSpec as P

F32, BF16 = jnp.float32, jnp.bfloat16
MESH = pl.DeviceIdType.MESH
KC = 512
NC = 256
XS = 4
WS = 6
RR = 6
SS = 3
LAG1, LAG2, LAG3 = 1, 3, 5
OWN, SIB, RT, RTS, FAR, FARS, LF, LFS = range(8)


def dot(a, b):
    return jnp.dot(a, b, preferred_element_type=F32)


def kernel(sizes, meta, x_hbm, wg, wu, wd, y_hbm, acc, xg, wbuf, z32, zb, disp, comb, metas, ssend, srecv, fsend, frecv,
           nsend, nrecv, yst, wsem, osem, ag_s, ag_r, m_s, m_r, sib_s, sib_r, f_s, f_r, n_s, n_r, ysem):
    tokens, d, ff, experts, slots, chips = sizes
    rows = experts * slots
    group = 2 * chips
    half = tokens // 2
    nk, nn = d // KC, d // NC
    nb_ff = ff // NC
    me = lax.axis_index("ep")
    chip, core = me // 2, me % 2

    def peer(rel):
        return {"ep": ((chip + rel // 2) % chips) * 2 + (core + rel % 2) % 2}

    def back(rel):
        return ((chips - rel // 2) % chips) * 2 + rel % 2

    first_down = nk * experts * 2

    def gate_up_copy(k, u, i):
        e, m = u // 2, u % 2
        b = i % WS
        w = (wg, wu)[m]
        return pltpu.make_async_copy(w.at[e, pl.ds(k * KC, KC), :], wbuf.at[b], wsem.at[b])

    def down_start(n, q, i):
        b = i % WS
        for p in range(2):
            for kb in range(nb_ff):
                pltpu.make_async_copy(
                    wd.at[2 * q + p, pl.ds(kb * NC, NC), pl.ds(n * NC, NC)],
                    wbuf.at[b, pl.ds(p * NC, NC), pl.ds(kb * NC, NC)],
                    wsem.at[b],
                ).start()

    def weights_wait(i):
        b = i % WS
        pltpu.make_async_copy(wbuf.at[b], wbuf.at[b], wsem.at[b]).wait()

    def block(k, rel, lo=0, n=tokens):
        return xg.at[pl.ds((k % XS) * (group * tokens) + rel * tokens + lo, n)]

    def own_copy(k):
        return pltpu.make_async_copy(x_hbm.at[:, pl.ds(k * KC, KC)], block(k, OWN), osem.at[k % XS])

    KINDS = [
        (OWN, LF, RT, 0, half),
        (OWN, RT, LF, half, half),
        (OWN, LF, RT, half, half),
        (OWN, RT, LF, 0, half),
        (OWN, SIB, SIB, 0, tokens),
        (LF, LFS, SIB, 0, tokens),
        (RT, RTS, SIB, 0, tokens),
        (LF, FAR, RT, 0, half),
        (RT, FAR, LF, half, half),
        (FAR, FARS, SIB, 0, half),
        (FAR, FARS, SIB, half, half),
    ]

    def ag(t, k):
        src, dst, to, lo, n = KINDS[t]
        s = k % XS
        return pltpu.make_async_remote_copy(
            src_ref=block(k, src, lo, n), dst_ref=block(k, dst, lo, n), send_sem=ag_s.at[t, s], recv_sem=ag_r.at[t, s],
            device_id=peer(to), device_id_type=MESH)

    def near_start(k):
        for t in (0, 1, 2, 3, 4):
            ag(t, k).start()

    def forward(k):
        for t, f in ((0, 7), (1, 8)):
            ag(t, k).wait_recv()
            ag(f, k).start()
        for t, f in ((2, 5), (3, 6)):
            ag(t, k).wait_recv()
            ag(f, k).start()

    def far_forward(k):
        for t, f in ((7, 9), (8, 10)):
            ag(t, k).wait_recv()
            ag(f, k).start()

    def sends_wait(k):
        for t in range(len(KINDS)):
            ag(t, k).wait_send()

    def meta_copy(rel):
        return pltpu.make_async_remote_copy(
            src_ref=meta, dst_ref=metas.at[back(rel)], send_sem=m_s.at[rel], recv_sem=m_r.at[back(rel)],
            device_id=peer(rel), device_id_type=MESH)

    for k in range(3):
        own_copy(k).start()
    for i in range(WS - 1):
        gate_up_copy(0, i, i).start()
    barrier = pltpu.get_barrier_semaphore()
    for rel in range(1, group):
        pl.semaphore_signal(barrier, inc=1, device_id=peer(rel), device_id_type=MESH)
    pl.semaphore_wait(barrier, group - 1)
    for rel in range(1, group):
        meta_copy(rel).start()
    own_copy(0).wait()
    near_start(0)
    metas[OWN] = meta[...]

    def zero(i, _):
        for e in range(experts):
            acc[e, i] = jnp.zeros(acc.shape[2:], F32)
        return 0

    lax.fori_loop(0, 2 * nb_ff, zero, 0)
    for rel in range(1, group):
        meta_copy(back(rel)).wait_recv()
    row_id = (lax.broadcasted_iota(jnp.int32, (rows, tokens), 0) + me * rows).astype(F32)

    def build_disp(r, _):
        m = metas[r]
        hit = jnp.zeros((rows, tokens), F32)
        for j in range(m.shape[0] // 2):
            hit = jnp.where(row_id == m[j:j + 1, :], 1.0, hit)
        disp[r] = hit.astype(BF16)
        return 0

    def build_comb(r, _):
        m = metas[r]
        top = m.shape[0] // 2
        g = jnp.zeros((rows, tokens), F32)
        for j in range(top):
            g = jnp.where(row_id == m[j:j + 1, :], m[top + j:top + j + 1, :], g)
        comb[r] = g.T.astype(BF16)
        return 0

    lax.fori_loop(0, group, build_disp, 0)
    forward(0)
    own_copy(1).wait()
    near_start(1)
    lax.fori_loop(0, group, build_comb, 0)
    far_forward(0)
    own_copy(2).wait()
    near_start(2)
    for rel in range(1, group):
        meta_copy(rel).wait_send()

    def gather(k):
        for t in (4, 5, 6, 9, 10):
            ag(t, k).wait_recv()
        for r in range(group):
            z = dot(disp[r], block(k, r)[...])
            for e in range(experts):
                z32[e, r * slots:(r + 1) * slots, :] = z[e * slots:(e + 1) * slots]

    def step(k, u, last):
        e, m = u // 2, u % 2
        i = k * (2 * experts) + u
        ahead = u + WS - 1
        if ahead < 2 * experts:
            gate_up_copy(k, ahead, i + WS - 1).start()
        elif not last:
            gate_up_copy(k + 1, ahead - 2 * experts, i + WS - 1).start()
        else:
            down_start((ahead - 2 * experts) // (experts // 2), (ahead - 2 * experts) % (experts // 2), i + WS - 1)
        weights_wait(i)
        b = i % WS
        if m == 0:
            zb[e % 2] = z32[e].astype(BF16)
        for nb in range(nb_ff):
            out = acc[e, m * nb_ff + nb] + dot(zb[e % 2], wbuf[b, :, nb * NC:(nb + 1) * NC])
            if last and m == 1:
                h = (jax.nn.silu(acc[e, nb]) * out).astype(BF16)
                at = (nb % 2) * NC
                xg[(e * (nb_ff // 2) + nb // 2) * (group * slots):(e * (nb_ff // 2) + nb // 2 + 1) * (group * slots),
                   at:at + NC] = h
            else:
                acc[e, m * nb_ff + nb] = out

    def chunk(k, _):
        @pl.when(k + 3 < nk)
        def _():
            own_copy(k + 3).start()

        gather(k)
        for u in range(2 * experts):
            step(k, u, False)
            if u == 3:
                sends_wait(k)
                forward(k + 1)

                @pl.when(k + 3 < nk)
                def _():
                    own_copy(k + 3).wait()
                    near_start(k + 3)
            if u == 11:
                far_forward(k + 1)
        return 0

    lax.fori_loop(0, nk - 1, chunk, 0)
    gather(nk - 1)
    sends_wait(nk - 1)
    for u in range(2 * experts):
        step(nk - 1, u, True)

    def sib_copy(m):
        return pltpu.make_async_remote_copy(
            src_ref=ssend.at[m % 2], dst_ref=srecv.at[m % 4], send_sem=sib_s.at[m % 2], recv_sem=sib_r.at[m % 4],
            device_id=peer(SIB), device_id_type=MESH)

    def far_copy(m, way):
        return pltpu.make_async_remote_copy(
            src_ref=fsend.at[m % SS, way], dst_ref=frecv.at[m % RR, way], send_sem=f_s.at[way, m % SS],
            recv_sem=f_r.at[way, m % RR], device_id=peer((RT, LF)[way]), device_id_type=MESH)

    def near_copy(m, way):
        return pltpu.make_async_remote_copy(
            src_ref=nsend.at[m % SS, way], dst_ref=nrecv.at[m % RR, way], send_sem=n_s.at[way, m % SS],
            recv_sem=n_r.at[way, m % RR], device_id=peer((RT, LF)[way]), device_id_type=MESH)

    def y_copy(m):
        return pltpu.make_async_copy(yst.at[m % 2], y_hbm.at[:, pl.ds(m * NC, NC)], ysem.at[m % 2])

    pairs = experts // 2
    total_pairs = nn * pairs

    def down(n):
        for e in range(experts):
            q = e // 2
            i = first_down + n * pairs + q
            b = i % WS
            if e % 2 == 0:
                ahead = q + WS - 1

                @pl.when(n * pairs + ahead < total_pairs)
                def _():
                    down_start(n + ahead // pairs, ahead % pairs, i + WS - 1)

                weights_wait(i)
            out = None
            for kb in range(nb_ff):
                at = (e * (nb_ff // 2) + kb // 2) * (group * slots)
                t = dot(xg[at:at + group * slots, (kb % 2) * NC:(kb % 2 + 1) * NC],
                        wbuf[b, (e % 2) * NC:(e % 2 + 1) * NC, kb * NC:(kb + 1) * NC])
                out = t if out is None else out + t
            z32[e, :, :NC] = out
        for r in range(group):
            rhs = z32[:, r * slots:(r + 1) * slots, :NC].reshape(rows, NC).astype(BF16)
            p = dot(comb[r], rhs)
            if r % 2:
                ssend[n % 2, r // 2] = p.astype(BF16)
            else:
                acc[n % 8, r // 2, :tokens, :] = p
        sib_copy(n).start()

    def to_far(m):
        sib_copy(m).wait_recv()
        s = m % 8
        far = acc[s, 2, :tokens, :] + srecv[m % 4, 2].astype(F32)
        fsend[m % SS, 0] = far[:half].astype(BF16)
        fsend[m % SS, 1] = far[half:].astype(BF16)
        for way in range(2):
            far_copy(m, way).start()
        for c in (0, 1, 3):
            acc[s, c, :tokens, :] = acc[s, c, :tokens, :] + srecv[m % 4, c].astype(F32)
        sib_copy(m).wait_send()

    def to_near(m):
        s = m % 8
        far_copy(m, 0).wait_recv()
        nsend[m % SS, 0, :half] = (acc[s, 1, :half, :] + frecv[m % RR, 0].astype(F32)).astype(BF16)
        nsend[m % SS, 0, half:] = acc[s, 1, half:tokens, :].astype(BF16)
        near_copy(m, 0).start()
        far_copy(m, 1).wait_recv()
        nsend[m % SS, 1, :half] = acc[s, 3, :half, :].astype(BF16)
        nsend[m % SS, 1, half:] = (acc[s, 3, half:tokens, :] + frecv[m % RR, 1].astype(F32)).astype(BF16)
        near_copy(m, 1).start()
        for way in range(2):
            far_copy(m, way).wait_send()

    def finish(m):
        for way in range(2):
            near_copy(m, way).wait_recv()

        @pl.when(m >= 2)
        def _():
            y_copy(m - 2).wait()

        s = m % 8
        total = acc[s, 0, :tokens, :] + nrecv[m % RR, 0].astype(F32) + nrecv[m % RR, 1].astype(F32)
        yst[m % 2] = total.astype(BF16)
        y_copy(m).start()
        for way in range(2):
            near_copy(m, way).wait_send()

    def columns(n, _):
        @pl.when(n < nn)
        def _():
            down(n)

        for lag, stage in ((LAG1, to_far), (LAG2, to_near), (LAG3, finish)):
            @pl.when((n >= lag) & (n < nn + lag))
            def _(lag=lag, stage=stage):
                stage(n - lag)
        return 0

    lax.fori_loop(0, nn + LAG3, columns, 0)
    for m in (nn - 2, nn - 1):
        y_copy(m).wait()


def solution(mesh):
    def body(x, expert, slot, gate, w_gate, w_up, w_down):
        x, expert, slot, gate = (v.reshape(v.shape[2:]) for v in (x, expert, slot, gate))
        tokens, d = x.shape
        top = expert.shape[1]
        experts, _, ff = w_gate.shape
        group = mesh.shape["ep"]
        chips = group // 2
        slots = 5 * tokens * top // (4 * experts * group)
        rows, all_rows = experts * slots, group * slots
        place = jnp.where(slot < slots, expert * slots + slot, -1).astype(F32)
        meta = jnp.concatenate([place.T, gate.astype(BF16).astype(F32).T], axis=0)
        any_, vmem = pl.BlockSpec(memory_space=pl.ANY), pl.BlockSpec(memory_space=pltpu.VMEM)
        dma, half = pltpu.SemaphoreType.DMA, tokens // 2
        y = pl.pallas_call(
            functools.partial(kernel, (tokens, d, ff, experts, slots, chips)),
            out_shape=jax.ShapeDtypeStruct((tokens, d), BF16),
            in_specs=[vmem, any_, any_, any_, any_],
            out_specs=any_,
            scratch_shapes=[
                pltpu.VMEM((experts, 2 * ff // NC, all_rows, NC), F32),
                pltpu.VMEM((XS * group * tokens, KC), BF16),
                pltpu.VMEM((WS, KC, ff), BF16),
                pltpu.VMEM((experts, all_rows, KC), F32),
                pltpu.VMEM((2, all_rows, KC), BF16),
                pltpu.VMEM((group, rows, tokens), BF16),
                pltpu.VMEM((group, tokens, rows), BF16),
                pltpu.VMEM((group, 2 * top, tokens), F32),
                pltpu.VMEM((2, chips, tokens, NC), BF16),
                pltpu.VMEM((4, chips, tokens, NC), BF16),
                pltpu.VMEM((SS, 2, half, NC), BF16),
                pltpu.VMEM((RR, 2, half, NC), BF16),
                pltpu.VMEM((SS, 2, tokens, NC), BF16),
                pltpu.VMEM((RR, 2, tokens, NC), BF16),
                pltpu.VMEM((2, tokens, NC), BF16),
                dma((WS,)), dma((XS,)), dma((11, XS)), dma((11, XS)), dma((group,)), dma((group,)),
                dma((2,)), dma((4,)), dma((2, SS)), dma((2, RR)), dma((2, SS)), dma((2, RR)), dma((2,)),
            ],
            compiler_params=pltpu.CompilerParams(
                collective_id=0, has_side_effects=True, vmem_limit_bytes=67043328),
            name="moe",
        )(meta, x, w_gate, w_up, w_down)
        return y.reshape(1, 1, tokens, d)

    tok = P("dp", "ep", None, None)
    w = P("ep", None, None)
    return jax.shard_map(body, mesh=mesh, in_specs=(tok, tok, tok, tok, w, w, w), out_specs=tok, check_vma=False)
```

time: 681 us -> 207 us (0.30)
  blocking collectives: 238 us -> 0 us
  waiting for transfers between devices: 219 us -> 0 us
  Pallas kernels: 0 us -> 201 us
  matrix products: 185 us -> 0 us
  local copies, waits for them, and re-layouts: 31.3 us -> 3.13 us
    another operation x1 -> x0, blocking collectives: 238 us -> none  [placed(): return lax.with_sharding_constraint(v, NamedSharding(mesh, P(*spec)))]
    another operation x1 -> x0, waiting for transfers between devices: 219 us -> none  [placed(): return lax.with_sharding_constraint(v, NamedSharding(mesh, P(*spec)))]
    pallas_call x0 -> x1, Pallas kernels: none -> 201 us  [body(): pl.pallas_call(functools.partial(kernel, (tokens, d, ff, experts, slots,...]
    dot_general x7 -> x0, matrix products: 185 us -> none  [einsum(): return jnp.einsum(form, a.astype(jnp.float32), b.astype(jnp.float32))]
    another operation x1 -> x0, local copies, waits for them, and re-layouts: 17.5 us -> none  [placed(): return lax.with_sharding_constraint(v, NamedSharding(mesh, P(*spec)))]
    convert_element_type x3 -> x0, local copies, waits for them, and re-layouts: 11.4 us -> none  [the longest x1 5.62 us: step(): einsum('abtke,abtkc->abtec', to_expert, to_slot).astype(jnp.bfloat16)]
  transfers between devices with their start and end apart: 1 -> 0, of which waited for: 1 -> 0; matrix products, arithmetic and copies ran while one was open for 1% -> 0% of each run, Pallas kernels for 0% -> 0%
where the time goes in v1:
time: 207 us
  Pallas kernels  201 us (97%)
  local copies, waits for them, and re-layouts  3.13 us (2%)
    pallas_call x1, Pallas kernels, body(): pl.pallas_call(functools.partial(kernel, (tokens, d, ff, experts, slots,...  201 us

profile of v1, /device:TPU:112, one launch (start us, length us, event | category | flops | bytes accessed | tf_op | source)
XLA Modules:
  0.0 206.5 jit_solution(11625283618384606860)
XLA Ops:
  0.0 0.7 convert_bitcast_fusion.1
  0.7 0.7 convert_bitcast_fusion
  1.4 0.6 pad_maximum_fusion.meta
  2.0 201.4 %moe.1 = bf16[256,4096]{1,0:T(8,128)(2,1)} custom-call(f32[16,256]{1,0:T(8,128)} %pad_maximum_fusion.meta, bf16[256,4096]{1,0:T(8,128)(2,1)} %bitcast.12, bf16[8,4096,1536]{2,1,0:T(8,128)(2,1)} %wg.1, bf16[8,4096,1536]{2,1,0:T(8,128)(2,1)} %wu.1, bf16[8,1536,4096]{2,1,0:T(8,128)(2,1)} %wd.1), custom_call_target="tpu_custom_call" | custom-call | tf_op jit(solution)/shard_map/moe/pallas_call | solution.py:348
  203.4 3.1 %copy.9 = bf16[1,1,256,4096]{3,2,1,0:T(8,128)(2,1)} copy(bf16[1,1,256,4096]{3,2,1,0:T(8,128)(2,1)} %bitcast.11) | data formatting | bytes 4194304

commit v2 on v1

--- a/solution.py
+++ b/solution.py
@@ -14,8 +14,8 @@
 XS = 4
 WS = 6
 RR = 6
-SS = 3
-LAG1, LAG2, LAG3 = 1, 3, 5
+SS = 4
+LAG1, LAG2, LAG3 = 1, 2, 5
 OWN, SIB, RT, RTS, FAR, FARS, LF, LFS = range(8)
 
 
@@ -23,7 +23,7 @@
     return jnp.dot(a, b, preferred_element_type=F32)
 
 
-def kernel(sizes, meta, x_hbm, wg, wu, wd, y_hbm, acc, xg, wbuf, z32, zb, disp, comb, metas, ssend, srecv, fsend, frecv,
+def kernel(sizes, expert, slot, gate, x_hbm, wg, wu, wd, y_hbm, acc, xg, wbuf, z32, zb, disp, comb, places, gates, ssend, srecv, fsend, frecv,
            nsend, nrecv, yst, wsem, osem, ag_s, ag_r, m_s, m_r, sib_s, sib_r, f_s, f_r, n_s, n_r, ysem):
     tokens, d, ff, experts, slots, chips = sizes
     rows = experts * slots
@@ -97,6 +97,8 @@
         for t, f in ((0, 7), (1, 8)):
             ag(t, k).wait_recv()
             ag(f, k).start()
+
+    def share(k):
         for t, f in ((2, 5), (3, 6)):
             ag(t, k).wait_recv()
             ag(f, k).start()
@@ -110,24 +112,33 @@
         for t in range(len(KINDS)):
             ag(t, k).wait_send()
 
-    def meta_copy(rel):
-        return pltpu.make_async_remote_copy(
-            src_ref=meta, dst_ref=metas.at[back(rel)], send_sem=m_s.at[rel], recv_sem=m_r.at[back(rel)],
+    def place_copy(rel):
+        return pltpu.make_async_remote_copy(
+            src_ref=places.at[OWN], dst_ref=places.at[back(rel)], send_sem=m_s.at[0, rel], recv_sem=m_r.at[0, back(rel)],
             device_id=peer(rel), device_id_type=MESH)
 
-    for k in range(3):
+    def gate_copy(rel):
+        return pltpu.make_async_remote_copy(
+            src_ref=gates.at[OWN], dst_ref=gates.at[back(rel)], send_sem=m_s.at[1, rel], recv_sem=m_r.at[1, back(rel)],
+            device_id=peer(rel), device_id_type=MESH)
+
+    for k in range(2):
         own_copy(k).start()
-    for i in range(WS - 1):
+    for i in range(WS - 2):
         gate_up_copy(0, i, i).start()
     barrier = pltpu.get_barrier_semaphore()
     for rel in range(1, group):
         pl.semaphore_signal(barrier, inc=1, device_id=peer(rel), device_id_type=MESH)
+    places[OWN] = jnp.where(slot[...] < slots, expert[...] * slots + slot[...], -1).astype(F32)
+    gates[OWN] = gate[...].astype(BF16).astype(F32)
+    own_copy(0).wait()
     pl.semaphore_wait(barrier, group - 1)
+    for t in (0, 1):
+        ag(t, 0).start()
     for rel in range(1, group):
-        meta_copy(rel).start()
-    own_copy(0).wait()
-    near_start(0)
-    metas[OWN] = meta[...]
+        place_copy(rel).start()
+    for t in (2, 3, 4):
+        ag(t, 0).start()
 
     def zero(i, _):
         for e in range(experts):
@@ -135,37 +146,36 @@
         return 0
 
     lax.fori_loop(0, 2 * nb_ff, zero, 0)
+    forward(0)
+    own_copy(1).wait()
+    near_start(1)
     for rel in range(1, group):
-        meta_copy(back(rel)).wait_recv()
+        gate_copy(rel).start()
+    for rel in range(1, group):
+        place_copy(back(rel)).wait_recv()
     row_id = (lax.broadcasted_iota(jnp.int32, (rows, tokens), 0) + me * rows).astype(F32)
 
     def build_disp(r, _):
-        m = metas[r]
+        m = places[r]
         hit = jnp.zeros((rows, tokens), F32)
-        for j in range(m.shape[0] // 2):
+        for j in range(m.shape[0]):
             hit = jnp.where(row_id == m[j:j + 1, :], 1.0, hit)
         disp[r] = hit.astype(BF16)
         return 0
 
-    def build_comb(r, _):
-        m = metas[r]
-        top = m.shape[0] // 2
+    def build_comb(r):
+        m, w = places[r], gates[r]
+        row = (lax.broadcasted_iota(jnp.int32, (rows, tokens), 0) + me * rows).astype(F32)
         g = jnp.zeros((rows, tokens), F32)
-        for j in range(top):
-            g = jnp.where(row_id == m[j:j + 1, :], m[top + j:top + j + 1, :], g)
+        for j in range(m.shape[0]):
+            g = jnp.where(row == m[j:j + 1, :], w[j:j + 1, :], g)
         comb[r] = g.T.astype(BF16)
-        return 0
 
     lax.fori_loop(0, group, build_disp, 0)
-    forward(0)
-    own_copy(1).wait()
-    near_start(1)
-    lax.fori_loop(0, group, build_comb, 0)
+    share(0)
     far_forward(0)
-    own_copy(2).wait()
-    near_start(2)
     for rel in range(1, group):
-        meta_copy(rel).wait_send()
+        place_copy(rel).wait_send()
 
     def gather(k):
         for t in (4, 5, 6, 9, 10):
@@ -178,14 +188,18 @@
     def step(k, u, last):
         e, m = u // 2, u % 2
         i = k * (2 * experts) + u
-        ahead = u + WS - 1
-        if ahead < 2 * experts:
-            gate_up_copy(k, ahead, i + WS - 1).start()
-        elif not last:
-            gate_up_copy(k + 1, ahead - 2 * experts, i + WS - 1).start()
-        else:
-            down_start((ahead - 2 * experts) // (experts // 2), (ahead - 2 * experts) % (experts // 2), i + WS - 1)
-        weights_wait(i)
+        if m == 0:
+            for v in range(2):
+                ahead = u + v + WS - 2
+                if ahead < 2 * experts:
+                    gate_up_copy(k, ahead, i + v + WS - 2).start()
+                elif not last:
+                    gate_up_copy(k + 1, ahead - 2 * experts, i + v + WS - 2).start()
+                else:
+                    q = ahead - 2 * experts
+                    down_start(q // (experts // 2), q % (experts // 2), i + v + WS - 2)
+            weights_wait(i)
+            weights_wait(i + 1)
         b = i % WS
         if m == 0:
             zb[e % 2] = z32[e].astype(BF16)
@@ -200,9 +214,9 @@
                 acc[e, m * nb_ff + nb] = out
 
     def chunk(k, _):
-        @pl.when(k + 3 < nk)
+        @pl.when(k + 2 < nk)
         def _():
-            own_copy(k + 3).start()
+            own_copy(k + 2).start()
 
         gather(k)
         for u in range(2 * experts):
@@ -211,17 +225,30 @@
                 sends_wait(k)
                 forward(k + 1)
 
-                @pl.when(k + 3 < nk)
+                @pl.when(k + 2 < nk)
                 def _():
-                    own_copy(k + 3).wait()
-                    near_start(k + 3)
-            if u == 11:
+                    own_copy(k + 2).wait()
+                    near_start(k + 2)
+
+            if u == 7:
+                share(k + 1)
+
+                @pl.when(k == 0)
+                def _():
+                    for rel in range(1, group):
+                        gate_copy(back(rel)).wait_recv()
+                        gate_copy(rel).wait_send()
+
+                build_comb(k)
+            if u == 13:
                 far_forward(k + 1)
         return 0
 
     lax.fori_loop(0, nk - 1, chunk, 0)
     gather(nk - 1)
     sends_wait(nk - 1)
+    for r in range(nk - 1, group):
+        build_comb(r)
     for u in range(2 * experts):
         step(nk - 1, u, True)
 
@@ -246,17 +273,17 @@
     pairs = experts // 2
     total_pairs = nn * pairs
 
-    def down(n):
-        for e in range(experts):
+    def down(n, first, last):
+        for e in range(first, last):
             q = e // 2
             i = first_down + n * pairs + q
             b = i % WS
             if e % 2 == 0:
-                ahead = q + WS - 1
+                ahead = q + WS - 2
 
                 @pl.when(n * pairs + ahead < total_pairs)
                 def _():
-                    down_start(n + ahead // pairs, ahead % pairs, i + WS - 1)
+                    down_start(n + ahead // pairs, ahead % pairs, i + WS - 2)
 
                 weights_wait(i)
             out = None
@@ -266,6 +293,8 @@
                         wbuf[b, (e % 2) * NC:(e % 2 + 1) * NC, kb * NC:(kb + 1) * NC])
                 out = t if out is None else out + t
             z32[e, :, :NC] = out
+
+    def combine(n):
         for r in range(group):
             rhs = z32[:, r * slots:(r + 1) * slots, :NC].reshape(rows, NC).astype(BF16)
             p = dot(comb[r], rhs)
@@ -318,12 +347,17 @@
     def columns(n, _):
         @pl.when(n < nn)
         def _():
-            down(n)
+            down(n, 0, experts // 2)
 
         for lag, stage in ((LAG1, to_far), (LAG2, to_near), (LAG3, finish)):
             @pl.when((n >= lag) & (n < nn + lag))
             def _(lag=lag, stage=stage):
                 stage(n - lag)
+
+        @pl.when(n < nn)
+        def _():
+            down(n, experts // 2, experts)
+            combine(n)
         return 0
 
     lax.fori_loop(0, nn + LAG3, columns, 0)
@@ -341,14 +375,12 @@
         chips = group // 2
         slots = 5 * tokens * top // (4 * experts * group)
         rows, all_rows = experts * slots, group * slots
-        place = jnp.where(slot < slots, expert * slots + slot, -1).astype(F32)
-        meta = jnp.concatenate([place.T, gate.astype(BF16).astype(F32).T], axis=0)
         any_, vmem = pl.BlockSpec(memory_space=pl.ANY), pl.BlockSpec(memory_space=pltpu.VMEM)
         dma, half = pltpu.SemaphoreType.DMA, tokens // 2
         y = pl.pallas_call(
             functools.partial(kernel, (tokens, d, ff, experts, slots, chips)),
             out_shape=jax.ShapeDtypeStruct((tokens, d), BF16),
-            in_specs=[vmem, any_, any_, any_, any_],
+            in_specs=[vmem, vmem, vmem, any_, any_, any_, any_],
             out_specs=any_,
             scratch_shapes=[
                 pltpu.VMEM((experts, 2 * ff // NC, all_rows, NC), F32),
@@ -358,7 +390,8 @@
                 pltpu.VMEM((2, all_rows, KC), BF16),
                 pltpu.VMEM((group, rows, tokens), BF16),
                 pltpu.VMEM((group, tokens, rows), BF16),
-                pltpu.VMEM((group, 2 * top, tokens), F32),
+                pltpu.VMEM((group, top, tokens), F32),
+                pltpu.VMEM((group, top, tokens), F32),
                 pltpu.VMEM((2, chips, tokens, NC), BF16),
                 pltpu.VMEM((4, chips, tokens, NC), BF16),
                 pltpu.VMEM((SS, 2, half, NC), BF16),
@@ -366,13 +399,13 @@
                 pltpu.VMEM((SS, 2, tokens, NC), BF16),
                 pltpu.VMEM((RR, 2, tokens, NC), BF16),
                 pltpu.VMEM((2, tokens, NC), BF16),
-                dma((WS,)), dma((XS,)), dma((11, XS)), dma((11, XS)), dma((group,)), dma((group,)),
+                dma((WS,)), dma((XS,)), dma((11, XS)), dma((11, XS)), dma((2, group)), dma((2, group)),
                 dma((2,)), dma((4,)), dma((2, SS)), dma((2, RR)), dma((2, SS)), dma((2, RR)), dma((2,)),
             ],
             compiler_params=pltpu.CompilerParams(
                 collective_id=0, has_side_effects=True, vmem_limit_bytes=67043328),
             name="moe",
-        )(meta, x, w_gate, w_up, w_down)
+        )(expert.T, slot.T, gate.T, x, w_gate, w_up, w_down)
         return y.reshape(1, 1, tokens, d)
 
     tok = P("dp", "ep", None, None)

time: 207 us -> 190 us (0.918)
  Pallas kernels: 201 us -> 186 us
    pallas_call x1, Pallas kernels: 201 us -> 186 us  [body(): pl.pallas_call(functools.partial(kernel, (tokens, d, ff, experts, slots,...]
where the time goes in v2:
time: 190 us; the launch traced here: 189 us
  Pallas kernels  186 us (98%)
  local copies, waits for them, and re-layouts  3.13 us (2%)
    pallas_call x1, Pallas kernels, body(): pl.pallas_call(functools.partial(kernel, (tokens, d, ff, experts, slots,...  186 us

profile of v2, /device:TPU:112, one launch (start us, length us, event | category | flops | bytes accessed | tf_op | source)
XLA Modules:
  0.0 189.5 jit_solution(11496506793696775469)
XLA Ops:
  0.0 186.3 %moe.1 = bf16[256,4096]{1,0:T(8,128)(2,1)} custom-call(s32[8,256]{1,0:T(8,128)} %bitcast.13, s32[8,256]{1,0:T(8,128)} %bitcast.14, f32[8,256]{1,0:T(8,128)} %bitcast.15, bf16[256,4096]{1,0:T(8,128)(2,1)} %bitcast.12, bf16[8,4096,1536]{2,1,0:T(8,128)(2,1)} %wg.1, bf16[8,4096,1536]{2,1,0:T(8,128)(2,1)} %wu.1, bf16[8,1536,4096]{2,1,0:T(8,128)(2,1)} %wd.1), custom_call_target="tpu_custom_call" | custom-call | tf_op jit(solution)/shard_map/moe/pallas_call | solution.py:380
  186.3 3.1 %copy.9 = bf16[1,1,256,4096]{3,2,1,0:T(8,128)(2,1)} copy(bf16[1,1,256,4096]{3,2,1,0:T(8,128)(2,1)} %bitcast.11) | data formatting | bytes 4194304

commit v3 on v2

--- a/solution.py
+++ b/solution.py
@@ -173,17 +173,19 @@
 
     lax.fori_loop(0, group, build_disp, 0)
     share(0)
-    far_forward(0)
     for rel in range(1, group):
         place_copy(rel).wait_send()
+
+    def gather_from(k, r):
+        z = dot(disp[r], block(k, r)[...])
+        for e in range(experts):
+            z32[e, r * slots:(r + 1) * slots, :] = z[e * slots:(e + 1) * slots]
 
     def gather(k):
         for t in (4, 5, 6, 9, 10):
             ag(t, k).wait_recv()
         for r in range(group):
-            z = dot(disp[r], block(k, r)[...])
-            for e in range(experts):
-                z32[e, r * slots:(r + 1) * slots, :] = z[e * slots:(e + 1) * slots]
+            gather_from(k, r)
 
     def step(k, u, last):
         e, m = u // 2, u % 2
@@ -218,7 +220,6 @@
         def _():
             own_copy(k + 2).start()
 
-        gather(k)
         for u in range(2 * experts):
             step(k, u, False)
             if u == 3:
@@ -242,10 +243,21 @@
                 build_comb(k)
             if u == 13:
                 far_forward(k + 1)
+        gather(k + 1)
         return 0
 
+    ag(4, 0).wait_recv()
+    for r in (OWN, SIB, RT, LF):
+        gather_from(0, r)
+    far_forward(0)
+    ag(5, 0).wait_recv()
+    ag(6, 0).wait_recv()
+    for r in (LFS, RTS, FAR):
+        gather_from(0, r)
+    ag(9, 0).wait_recv()
+    ag(10, 0).wait_recv()
+    gather_from(0, FARS)
     lax.fori_loop(0, nk - 1, chunk, 0)
-    gather(nk - 1)
     sends_wait(nk - 1)
     for r in range(nk - 1, group):
         build_comb(r)
@@ -274,18 +286,18 @@
     total_pairs = nn * pairs
 
     def down(n, first, last):
+        i0 = first_down + n * pairs
+        for q in range(first // 2, last // 2):
+            ahead = q + WS - 2
+
+            @pl.when(n * pairs + ahead < total_pairs)
+            def _(q=q, ahead=ahead):
+                down_start(n + ahead // pairs, ahead % pairs, i0 + q + WS - 2)
+
+        for q in range(first // 2, last // 2):
+            weights_wait(i0 + q)
         for e in range(first, last):
-            q = e // 2
-            i = first_down + n * pairs + q
-            b = i % WS
-            if e % 2 == 0:
-                ahead = q + WS - 2
-
-                @pl.when(n * pairs + ahead < total_pairs)
-                def _():
-                    down_start(n + ahead // pairs, ahead % pairs, i + WS - 2)
-
-                weights_wait(i)
+            b = (i0 + e // 2) % WS
             out = None
             for kb in range(nb_ff):
                 at = (e * (nb_ff // 2) + kb // 2) * (group * slots)

time: 190 us -> 189 us (level)
  no operation moved by 1% of the time
where the time goes in v3:
time: 189 us
  Pallas kernels  186 us (98%)
  local copies, waits for them, and re-layouts  3.13 us (2%)
    pallas_call x1, Pallas kernels, body(): pl.pallas_call(functools.partial(kernel, (tokens, d, ff, experts, slots,...  186 us

profile of v3, /device:TPU:112, one launch (start us, length us, event | category | flops | bytes accessed | tf_op | source)
XLA Modules:
  0.0 188.7 jit_solution(3021815420034604113)
XLA Ops:
  0.0 185.5 %moe.1 = bf16[256,4096]{1,0:T(8,128)(2,1)} custom-call(s32[8,256]{1,0:T(8,128)} %bitcast.13, s32[8,256]{1,0:T(8,128)} %bitcast.14, f32[8,256]{1,0:T(8,128)} %bitcast.15, bf16[256,4096]{1,0:T(8,128)(2,1)} %bitcast.12, bf16[8,4096,1536]{2,1,0:T(8,128)(2,1)} %wg.1, bf16[8,4096,1536]{2,1,0:T(8,128)(2,1)} %wu.1, bf16[8,1536,4096]{2,1,0:T(8,128)(2,1)} %wd.1), custom_call_target="tpu_custom_call" | custom-call | tf_op jit(solution)/shard_map/moe/pallas_call | solution.py:392
  185.5 3.1 %copy.9 = bf16[1,1,256,4096]{3,2,1,0:T(8,128)(2,1)} copy(bf16[1,1,256,4096]{3,2,1,0:T(8,128)(2,1)} %bitcast.11) | data formatting | bytes 4194304
